TPU v7x, 128 devices: a whole 4x4x4 slice. The times are simulated.
128 devices in a mesh: gx: 8 (over y_lo, x), gy: 8 (over z, core), gz: 2 (over y_hi).
Axes of the slice: x: 4, y: 4 (y_hi: 2, y_lo: 2; y = y_hi * 2 + y_lo), z: 4, core: 2. Of those that a mesh axis runs over, the one named last changes fastest.
Arguments:
- blocks: int32 [131072, 4], P(('gx', 'gy', 'gz')), may hold values from 0 to 15, as said below
- coefficients: bfloat16 [131072, 4, 128], P(('gx', 'gy', 'gz')), may hold values from -80 to 80
- residuals: float32 [131072], P(('gx', 'gy', 'gz')), may hold values from -3000 to 3000
Outputs:
- factor: float32 [8, 2, 128, 8, 2, 128], P('gx', None, None, 'gy')
- solution: float32 [16, 128], replicated
Inputs may be any that keep to these rules, and one draw needn't show every extreme that they name: Each row names 4 different blocks.
All inputs are finite; a program needn't handle non-finite values.
Results may differ from a plain program's by a relative error of at most 0.0003.
Values sent between devices are 32-bit elements; how exact they have to be, the bound alone decides.
No kernel may reach another device: no remote copies, remote signals or barrier semaphores. Data moves between devices by JAX's collectives and lax.ppermute only.
A program may use at most 128 MiB of HBM per device.

v0:
```python
import jax
import jax.numpy as jnp
from jax import lax
from jax.sharding import PartitionSpec as P

G = 2048
BS = 128


def picked(x, axis, root):
    return lax.dynamic_index_in_dim(lax.all_gather(x, axis), root, 0, keepdims=False)


def laid_out(pieces, dim):
    shape = list(pieces.shape[1:])
    shape[dim] *= pieces.shape[0]
    return jnp.moveaxis(pieces, 0, dim).reshape(shape)


def copy_for_each(x, axis):
    size = lax.axis_size(axis)
    return lax.all_to_all(jnp.broadcast_to(x[None], (size, *x.shape)), axis, 0, 0, tiled=True)


def gather_directly(x, axis, dim):
    return laid_out(copy_for_each(x, axis), dim)


def on_device(blocks, coefficients, residuals):
    row_count = lax.axis_size("gx")
    col_count = lax.axis_size("gy")
    row_index = lax.axis_index("gx")
    col_index = lax.axis_index("gy")
    scale = 1.0 / (coefficients.shape[0] * row_count * col_count * lax.axis_size("gz"))
    width = coefficients.shape[2]
    nblock = G // BS
    per_dev = nblock // row_count
    target = (
        jnp.arange(per_dev, dtype=jnp.int32)[None, :] * row_count
        + jnp.arange(row_count, dtype=jnp.int32)[:, None]
    ).reshape(-1)
    placed = (blocks[:, :, None] == target[None, None, :]).astype(jnp.bfloat16)
    design = jnp.einsum("osz,osx->ozx", placed, coefficients, preferred_element_type=jnp.float32)
    design = design.astype(jnp.bfloat16).reshape(-1, row_count, per_dev, width)
    natural = (blocks[:, :, None] == jnp.arange(nblock, dtype=jnp.int32)[None, None, :]).astype(
        jnp.float32
    )
    weighted = coefficients.astype(jnp.float32) * residuals[:, None, None]
    rhs_local = (
        jnp.einsum("osb,osx->bx", natural, weighted, precision=lax.Precision.HIGHEST) * scale
    )
    rhs = lax.psum(rhs_local, ("gx", "gy", "gz"))
    row_span = min(row_count, (1 * lax.axis_size(("gx", "gy")) - 1) // col_count + 2)
    blockwise = (
        jnp.einsum("opix,oqjy->pqixjy", design, design, preferred_element_type=jnp.float32) * scale
    )
    blockwise = blockwise.reshape(row_span * col_count, per_dev, width, per_dev, width)
    summed = lax.psum_scatter(blockwise, ("gx", "gy"), scatter_dimension=0, tiled=True)
    summed = lax.psum(summed, "gz")
    matrix = summed.reshape(per_dev, width, per_dev, width)
    zero = jnp.zeros((), jnp.int32)
    block_ids = (
        jnp.arange(per_dev, dtype=jnp.int32)[None, :] * row_count
        + jnp.arange(row_count, dtype=jnp.int32)[:, None]
    )

    def factor_step(step, state):
        working, factor, pivots = state
        step_row = step % row_count
        step_local_row = step // row_count
        step_col = step % col_count
        step_local_col = step // col_count
        column = lax.dynamic_slice(
            working, (zero, zero, step_local_col, zero), (per_dev, width, 1, width)
        ).reshape(per_dev, width, width)
        row_raw = picked(column, "gy", step_col)
        whole = gather_directly(row_raw, "gx", 0).reshape(row_count, per_dev, width, width)
        own_diag = lax.dynamic_slice(
            whole, (step_row, step_local_row, zero, zero), (1, 1, width, width)
        ).reshape(width, width)
        chol = jnp.linalg.cholesky(own_diag)
        stacked = whole.transpose(3, 0, 1, 2).reshape(width, row_count * per_dev * width)
        solved = jax.scipy.linalg.solve_triangular(chol, stacked, lower=True)
        panel_all = solved.reshape(width, row_count, per_dev, width).transpose(1, 2, 3, 0)
        panel_all = jnp.where((block_ids > step)[:, :, None, None], panel_all, 0.0)
        row_panel = lax.dynamic_index_in_dim(panel_all, row_index, 0, keepdims=False)
        col_panel = lax.dynamic_index_in_dim(panel_all, col_index, 0, keepdims=False)
        working = working - jnp.einsum(
            "rxk,cyk->rxcy", row_panel, col_panel, precision=lax.Precision.HIGHEST
        )
        on_diag = (jnp.arange(per_dev, dtype=jnp.int32) == step_local_row) & (row_index == step_row)
        new_column = row_panel + jnp.where(on_diag[:, None, None], chol[None], 0.0)
        old_column = lax.dynamic_slice(
            factor, (zero, zero, step_local_col, zero), (per_dev, width, 1, width)
        ).reshape(per_dev, width, width)
        kept = jnp.where(col_index == step_col, new_column, old_column)
        factor = lax.dynamic_update_slice(
            factor, kept.reshape(per_dev, width, 1, width), (zero, zero, step_local_col, zero)
        )
        pivots = lax.dynamic_update_slice(pivots, chol[None], (step, zero, zero))
        return (working, factor, pivots)

    start_state = (matrix, jnp.zeros_like(matrix), jnp.zeros((nblock, width, width), jnp.float32))
    _, factor, pivots = lax.fori_loop(0, nblock, factor_step, start_state)
    shaped = factor.reshape(1, per_dev, width, 1, per_dev, width)
    across = lax.all_gather(shaped, "gy", axis=3, tiled=True)
    whole = lax.all_gather(across, "gx", axis=0, tiled=True)
    lower = whole.transpose(1, 0, 2, 4, 3, 5).reshape(nblock * width, nblock * width)
    middle = jax.scipy.linalg.solve_triangular(lower, rhs.reshape(-1), lower=True)
    answer = jax.scipy.linalg.solve_triangular(lower, middle, lower=True, trans=1)
    solution = answer.reshape(nblock, width)
    return (factor.reshape(1, per_dev, width, 1, per_dev, width), solution)


def solution(mesh):
    in_specs = (
        P(("gx", "gy", "gz"), None),
        P(("gx", "gy", "gz"), None, None),
        P(("gx", "gy", "gz")),
    )
    out_specs = (P("gx", None, None, "gy", None, None), P())
    return jax.shard_map(
        on_device, mesh=mesh, in_specs=in_specs, out_specs=out_specs, check_vma=False
    )
```

profile of v0, /device:TPU:1, one launch (start us, length us, event | category | flops | bytes accessed | tf_op | source)
XLA Modules:
  0.0 2133.1 jit_solution(3347520525819320981)
XLA Ops:
  25.3 16.4 copy.39
  42.0 311.7 %reduce-scatter.2.cloned.1.call-done = f32[1,2,128,2,128]{4,2,3,1,0:T(8,128)} async-done(((f32[64,2,128,2,128]{4,2,3,1,0:T(8,128)}), f32[1,2,128,2,128]{4,2,3,1,0:T(8,128)}) %reduce-scatter.2.cloned.1.call-update) | async-done | bytes 262160 | tf_op jit(solution)/shard_map/reduce_scatter | solution.py:58
  353.8 35.4 %all-reduce.2.cloned.1.call-done = f32[2,128,2,128]{3,1,2,0:T(8,128)} async-done(((f32[2,128,2,128]{3,1,2,0:T(8,128)}), f32[2,128,2,128]{3,1,2,0:T(8,128)}) %all-reduce.2.cloned.1.call-update) | async-done | bytes 262160 | tf_op jit(solution)/shard_map/psum | solution.py:59
  389.2 1176.2 %while.20 = (s32[]{:T(128)}, f32[2,128,2,128]{3,1,2,0:T(8,128)}, f32[2,128,2,128]{3,1,0,2:T(8,128)S(1)}, s32[]{:T(128)}, s32[]{:T(128)}, /*index=5*/s32[]{:T(128...) while((s32[]{:T(128)}, f32[2,128,2,128]{3,1,2,0:T(8,128)}, ...), condition=%wide.region_5.6_spmd.clone, body=%wide.region_2.5_spmd.clone.sunk | while | flops 503890112 | bytes 12519428 | solution.py:104
  391.0 25.2 %all-gather.13.cloned.1.call-done = f32[16,128,1,128]{3,1,2,0:T(8,128)} async-done(((f32[2,128,1,128]{3,1,2,0:T(8,128)}), f32[16,128,1,128]{3,1,2,0:T(8,128)}) %all-gather.13.cloned.1.call-update) | async-done | bytes 1048592 | tf_op jit(solution)/shard_map/while/body/eval_jaxpr/all_gather | solution.py:11
  423.0 15.8 all-to-all-done
  466.8 22.6 %all-gather.13.cloned.1.call-done = f32[16,128,1,128]{3,1,2,0:T(8,128)} async-done(((f32[2,128,1,128]{3,1,2,0:T(8,128)}), f32[16,128,1,128]{3,1,2,0:T(8,128)}) %all-gather.13.cloned.1.call-update) | async-done | bytes 1048592 | tf_op jit(solution)/shard_map/while/body/eval_jaxpr/all_gather | solution.py:11
  496.3 15.8 all-to-all-done
  540.0 22.6 %all-gather.13.cloned.1.call-done = f32[16,128,1,128]{3,1,2,0:T(8,128)} async-done(((f32[2,128,1,128]{3,1,2,0:T(8,128)}), f32[16,128,1,128]{3,1,2,0:T(8,128)}) %all-gather.13.cloned.1.call-update) | async-done | bytes 1048592 | tf_op jit(solution)/shard_map/while/body/eval_jaxpr/all_gather | solution.py:11
  569.5 15.8 all-to-all-done
  613.3 22.6 %all-gather.13.cloned.1.call-done = f32[16,128,1,128]{3,1,2,0:T(8,128)} async-done(((f32[2,128,1,128]{3,1,2,0:T(8,128)}), f32[16,128,1,128]{3,1,2,0:T(8,128)}) %all-gather.13.cloned.1.call-update) | async-done | bytes 1048592 | tf_op jit(solution)/shard_map/while/body/eval_jaxpr/all_gather | solution.py:11
  642.8 15.8 all-to-all-done
  686.5 22.9 %all-gather.13.cloned.1.call-done = f32[16,128,1,128]{3,1,2,0:T(8,128)} async-done(((f32[2,128,1,128]{3,1,2,0:T(8,128)}), f32[16,128,1,128]{3,1,2,0:T(8,128)}) %all-gather.13.cloned.1.call-update) | async-done | bytes 1048592 | tf_op jit(solution)/shard_map/while/body/eval_jaxpr/all_gather | solution.py:11
  716.4 15.8 all-to-all-done
  760.1 22.9 %all-gather.13.cloned.1.call-done = f32[16,128,1,128]{3,1,2,0:T(8,128)} async-done(((f32[2,128,1,128]{3,1,2,0:T(8,128)}), f32[16,128,1,128]{3,1,2,0:T(8,128)}) %all-gather.13.cloned.1.call-update) | async-done | bytes 1048592 | tf_op jit(solution)/shard_map/while/body/eval_jaxpr/all_gather | solution.py:11
  833.6 22.9 %all-gather.13.cloned.1.call-done = f32[16,128,1,128]{3,1,2,0:T(8,128)} async-done(((f32[2,128,1,128]{3,1,2,0:T(8,128)}), f32[16,128,1,128]{3,1,2,0:T(8,128)}) %all-gather.13.cloned.1.call-update) | async-done | bytes 1048592 | tf_op jit(solution)/shard_map/while/body/eval_jaxpr/all_gather | solution.py:11
  907.2 22.6 %all-gather.13.cloned.1.call-done = f32[16,128,1,128]{3,1,2,0:T(8,128)} async-done(((f32[2,128,1,128]{3,1,2,0:T(8,128)}), f32[16,128,1,128]{3,1,2,0:T(8,128)}) %all-gather.13.cloned.1.call-update) | async-done | bytes 1048592 | tf_op jit(solution)/shard_map/while/body/eval_jaxpr/all_gather | solution.py:11
  936.7 15.8 all-to-all-done
  980.5 22.9 %all-gather.13.cloned.1.call-done = f32[16,128,1,128]{3,1,2,0:T(8,128)} async-done(((f32[2,128,1,128]{3,1,2,0:T(8,128)}), f32[16,128,1,128]{3,1,2,0:T(8,128)}) %all-gather.13.cloned.1.call-update) | async-done | bytes 1048592 | tf_op jit(solution)/shard_map/while/body/eval_jaxpr/all_gather | solution.py:11
  1054.0 22.6 %all-gather.13.cloned.1.call-done = f32[16,128,1,128]{3,1,2,0:T(8,128)} async-done(((f32[2,128,1,128]{3,1,2,0:T(8,128)}), f32[16,128,1,128]{3,1,2,0:T(8,128)}) %all-gather.13.cloned.1.call-update) | async-done | bytes 1048592 | tf_op jit(solution)/shard_map/while/body/eval_jaxpr/all_gather | solution.py:11
  1127.3 22.9 %all-gather.13.cloned.1.call-done = f32[16,128,1,128]{3,1,2,0:T(8,128)} async-done(((f32[2,128,1,128]{3,1,2,0:T(8,128)}), f32[16,128,1,128]{3,1,2,0:T(8,128)}) %all-gather.13.cloned.1.call-update) | async-done | bytes 1048592 | tf_op jit(solution)/shard_map/while/body/eval_jaxpr/all_gather | solution.py:11
  1200.8 22.6 %all-gather.13.cloned.1.call-done = f32[16,128,1,128]{3,1,2,0:T(8,128)} async-done(((f32[2,128,1,128]{3,1,2,0:T(8,128)}), f32[16,128,1,128]{3,1,2,0:T(8,128)}) %all-gather.13.cloned.1.call-update) | async-done | bytes 1048592 | tf_op jit(solution)/shard_map/while/body/eval_jaxpr/all_gather | solution.py:11
  1274.1 22.6 %all-gather.13.cloned.1.call-done = f32[16,128,1,128]{3,1,2,0:T(8,128)} async-done(((f32[2,128,1,128]{3,1,2,0:T(8,128)}), f32[16,128,1,128]{3,1,2,0:T(8,128)}) %all-gather.13.cloned.1.call-update) | async-done | bytes 1048592 | tf_op jit(solution)/shard_map/while/body/eval_jaxpr/all_gather | solution.py:11
  1303.6 15.8 all-to-all-done
  1347.4 22.6 %all-gather.13.cloned.1.call-done = f32[16,128,1,128]{3,1,2,0:T(8,128)} async-done(((f32[2,128,1,128]{3,1,2,0:T(8,128)}), f32[16,128,1,128]{3,1,2,0:T(8,128)}) %all-gather.13.cloned.1.call-update) | async-done | bytes 1048592 | tf_op jit(solution)/shard_map/while/body/eval_jaxpr/all_gather | solution.py:11
  1420.6 22.6 %all-gather.13.cloned.1.call-done = f32[16,128,1,128]{3,1,2,0:T(8,128)} async-done(((f32[2,128,1,128]{3,1,2,0:T(8,128)}), f32[16,128,1,128]{3,1,2,0:T(8,128)}) %all-gather.13.cloned.1.call-update) | async-done | bytes 1048592 | tf_op jit(solution)/shard_map/while/body/eval_jaxpr/all_gather | solution.py:11
  1493.9 22.6 %all-gather.13.cloned.1.call-done = f32[16,128,1,128]{3,1,2,0:T(8,128)} async-done(((f32[2,128,1,128]{3,1,2,0:T(8,128)}), f32[16,128,1,128]{3,1,2,0:T(8,128)}) %all-gather.13.cloned.1.call-update) | async-done | bytes 1048592 | tf_op jit(solution)/shard_map/while/body/eval_jaxpr/all_gather | solution.py:11
  1566.2 25.3 %all-gather.11.cloned.1.call-done = f32[2,128,16,128]{3,1,0,2:T(8,128)} async-done(((f32[2,128,2,128]{3,1,0,2:T(8,128)}), f32[2,128,16,128]{3,1,0,2:T(8,128)}) %all-gather.11.cloned.1.call-update) | async-done | bytes 2097168 | tf_op jit(solution)/shard_map/all_gather | solution.py:106
  1599.6 214.9 %psum.15 = f32[16,128]{1,0:T(8,128)S(1)} all-reduce(f32[16,128]{1,0:T(8,128)S(1)} %fusion.19), channel_id=1, replica_groups=mesh['gx'=8,'gy'=8,'gz'=2] {'gx','gy','gz'}, use_global_device_ids=true, to_apply=%region_6.7 | all-reduce | flops 2048 | bytes 16384 | tf_op jit(solution)/shard_map/psum | solution.py:52
  1827.8 18.0 reshape.532
  1858.2 56.3 %while.19 = (s32[]{:T(128)}, f32[2048,2048]{1,0:T(8,128)}, s32[16,2]{0,1:T(2,128)S(1)}, f32[16,128,128]{2,1,0:T(8,128)}, s32[]{:T(128)}) while((s32[]{:T(128)}, f32[2048,2048]{1,0:T(8,128)}, s32[16,2]{0,1:T(2,128)S(1)}, f32[16,128,128]{2,1,0:T(8,128)}, s32[]{:T(128)}) %tuple.184), condition=%wide.while_cond, body=%wide.while_body.sunk | while | flops 2 | bytes 132705 | solution.py:110
  1914.5 157.9 %custom-call.28 = f32[16,128,128]{1,2,0:T(8,128)S(1)} custom-call(f32[16,128,128]{2,1,0:T(8,128)} %get-tuple-element.183), custom_call_target="InvertDiagBlocksLowerTriangular" | custom-call | tf_op jit(solution)/shard_map/jit(_solve_triangular)/triangular_solve | solution.py:110
  (573 shorter events, 860.1 us)
Async XLA Ops:
  7.2 346.6 %reduce-scatter.2.cloned.1.call-start = ((), (), s32[]{:S(2)}) async-start(), calls=%async_computation.2 | async-start | bytes 17039360 | tf_op jit(solution)/shard_map/reduce_scatter | solution.py:58
  41.8 347.4 %all-reduce.2.cloned.1.call-start = ((), (), s32[]{:S(2)}) async-start(), calls=%async_computation.3 | async-start | bytes 524288 | tf_op jit(solution)/shard_map/psum | solution.py:59
  389.2 26.9 %all-gather.13.cloned.1.call-start = ((), (), s32[]{:S(2)}) async-start(), calls=%async_computation.6 | async-start | bytes 1179648 | tf_op jit(solution)/shard_map/while/body/eval_jaxpr/all_gather | solution.py:11
  418.1 20.8 all-to-all-start
  465.1 24.3 %all-gather.13.cloned.1.call-start = ((), (), s32[]{:S(2)}) async-start(), calls=%async_computation.6 | async-start | bytes 1179648 | tf_op jit(solution)/shard_map/while/body/eval_jaxpr/all_gather | solution.py:11
  538.3 24.3 %all-gather.13.cloned.1.call-start = ((), (), s32[]{:S(2)}) async-start(), calls=%async_computation.6 | async-start | bytes 1179648 | tf_op jit(solution)/shard_map/while/body/eval_jaxpr/all_gather | solution.py:11
  564.6 20.8 all-to-all-start
  611.6 24.3 %all-gather.13.cloned.1.call-start = ((), (), s32[]{:S(2)}) async-start(), calls=%async_computation.6 | async-start | bytes 1179648 | tf_op jit(solution)/shard_map/while/body/eval_jaxpr/all_gather | solution.py:11
  637.9 20.8 all-to-all-start
  684.8 24.6 %all-gather.13.cloned.1.call-start = ((), (), s32[]{:S(2)}) async-start(), calls=%async_computation.6 | async-start | bytes 1179648 | tf_op jit(solution)/shard_map/while/body/eval_jaxpr/all_gather | solution.py:11
  758.4 24.6 %all-gather.13.cloned.1.call-start = ((), (), s32[]{:S(2)}) async-start(), calls=%async_computation.6 | async-start | bytes 1179648 | tf_op jit(solution)/shard_map/while/body/eval_jaxpr/all_gather | solution.py:11
  785.0 20.8 all-to-all-start
  832.0 24.6 %all-gather.13.cloned.1.call-start = ((), (), s32[]{:S(2)}) async-start(), calls=%async_computation.6 | async-start | bytes 1179648 | tf_op jit(solution)/shard_map/while/body/eval_jaxpr/all_gather | solution.py:11
  858.6 20.8 all-to-all-start
  905.5 24.3 %all-gather.13.cloned.1.call-start = ((), (), s32[]{:S(2)}) async-start(), calls=%async_computation.6 | async-start | bytes 1179648 | tf_op jit(solution)/shard_map/while/body/eval_jaxpr/all_gather | solution.py:11
  978.8 24.6 %all-gather.13.cloned.1.call-start = ((), (), s32[]{:S(2)}) async-start(), calls=%async_computation.6 | async-start | bytes 1179648 | tf_op jit(solution)/shard_map/while/body/eval_jaxpr/all_gather | solution.py:11
  1005.4 20.8 all-to-all-start
  1052.4 24.3 %all-gather.13.cloned.1.call-start = ((), (), s32[]{:S(2)}) async-start(), calls=%async_computation.6 | async-start | bytes 1179648 | tf_op jit(solution)/shard_map/while/body/eval_jaxpr/all_gather | solution.py:11
  1078.6 20.8 all-to-all-start
  1125.6 24.6 %all-gather.13.cloned.1.call-start = ((), (), s32[]{:S(2)}) async-start(), calls=%async_computation.6 | async-start | bytes 1179648 | tf_op jit(solution)/shard_map/while/body/eval_jaxpr/all_gather | solution.py:11
  1152.2 20.8 all-to-all-start
  1199.2 24.3 %all-gather.13.cloned.1.call-start = ((), (), s32[]{:S(2)}) async-start(), calls=%async_computation.6 | async-start | bytes 1179648 | tf_op jit(solution)/shard_map/while/body/eval_jaxpr/all_gather | solution.py:11
  1225.4 20.8 all-to-all-start
  1272.4 24.3 %all-gather.13.cloned.1.call-start = ((), (), s32[]{:S(2)}) async-start(), calls=%async_computation.6 | async-start | bytes 1179648 | tf_op jit(solution)/shard_map/while/body/eval_jaxpr/all_gather | solution.py:11
  1298.7 20.8 all-to-all-start
  1345.7 24.3 %all-gather.13.cloned.1.call-start = ((), (), s32[]{:S(2)}) async-start(), calls=%async_computation.6 | async-start | bytes 1179648 | tf_op jit(solution)/shard_map/while/body/eval_jaxpr/all_gather | solution.py:11
  1372.0 20.8 all-to-all-start
  1418.9 24.3 %all-gather.13.cloned.1.call-start = ((), (), s32[]{:S(2)}) async-start(), calls=%async_computation.6 | async-start | bytes 1179648 | tf_op jit(solution)/shard_map/while/body/eval_jaxpr/all_gather | solution.py:11
  1445.2 20.8 all-to-all-start
  1492.2 24.3 %all-gather.13.cloned.1.call-start = ((), (), s32[]{:S(2)}) async-start(), calls=%async_computation.6 | async-start | bytes 1179648 | tf_op jit(solution)/shard_map/while/body/eval_jaxpr/all_gather | solution.py:11
  1565.4 26.1 %all-gather.11.cloned.1.call-start = ((), (), s32[]{:S(2)}) async-start(), calls=%async_computation.5 | async-start | bytes 2359296 | tf_op jit(solution)/shard_map/all_gather | solution.py:106
  1566.2 250.1 %all-gather.9.cloned.1.call-start = ((), (), s32[]{:S(2)}) async-start(), calls=%async_computation.4 | async-start | bytes 18874368 | tf_op jit(solution)/shard_map/all_gather | solution.py:107
  (9 other events, 3707.0 us)
Sparse Core Ops, SparseCore 0:
  41.9 311.8 reduce-scatter.1
  356.2 32.9 all-reduce.1
  392.3 23.7 all-gather.12
  467.9 21.4 all-gather.12
  541.1 21.4 all-gather.12
  614.4 21.4 all-gather.12
  688.0 21.4 all-gather.12
  761.5 21.4 all-gather.12
  835.1 21.4 all-gather.12
  908.3 21.4 all-gather.12
  981.9 21.4 all-gather.12
  1055.1 21.4 all-gather.12
  1128.7 21.4 all-gather.12
  1202.0 21.4 all-gather.12
  1275.2 21.4 all-gather.12
  1348.5 21.4 all-gather.12
  1421.7 21.4 all-gather.12
  1495.0 21.4 all-gather.12
  1568.0 23.5 all-gather.10
  1595.8 170.8 all-gather.8
where the time goes:
time: 2140 us; the launch traced here: 2130 us
  waiting for transfers between devices  992 us (46%)
  other arithmetic  543 us (25%)
  blocking collectives  215 us (10%)
  local copies, waits for them, and re-layouts  170 us (8%)
  matrix products  116 us (5%)
  starting transfers between devices  79.4 us (4%)
    all_gather x16, waiting for transfers between devices, picked(): lax.all_gather(x, axis)  366 us
    reduce_scatter x1, waiting for transfers between devices, on_device(): lax.psum_scatter(blockwise, ('gx', 'gy'), scatter_dimension=0, tiled=True)  312 us
    all_to_all x16, waiting for transfers between devices, copy_for_each(): lax.all_to_all(jnp.broadcast_to(x[None], (size, *x.shape)), axis, 0, 0, t...  253 us
    psum x1, blocking collectives, on_device(): rhs = lax.psum(rhs_local, ('gx', 'gy', 'gz'))  215 us
    another operation x48, other arithmetic, factor_step(): chol = jnp.linalg.cholesky(own_diag)  199 us
    another operation x3, other arithmetic, on_device(): jax.scipy.linalg.solve_triangular(lower, middle, lower=True, trans=1)  170 us
    another operation x32, other arithmetic, factor_step(): solved = jax.scipy.linalg.solve_triangular(chol, stacked, lower=True)  168 us
    all_to_all x16, starting transfers between devices, copy_for_each(): lax.all_to_all(jnp.broadcast_to(x[None], (size, *x.shape)), axis, 0, 0, t...  78.3 us
  transfers between devices with their start and end apart: 36, of which 35 were waited for; matrix products, arithmetic and copies ran while one was open for 0% of the time, Pallas kernels for 0%

commit v1 on v0

--- a/solution.py
+++ b/solution.py
@@ -49,7 +49,7 @@
     rhs_local = (
         jnp.einsum("osb,osx->bx", natural, weighted, precision=lax.Precision.HIGHEST) * scale
     )
-    rhs = lax.psum(rhs_local, ("gx", "gy", "gz"))
+    rhs = jnp.sum(lax.all_gather(rhs_local, ("gx", "gy", "gz")), 0)
     row_span = min(row_count, (1 * lax.axis_size(("gx", "gy")) - 1) // col_count + 2)
     blockwise = (
         jnp.einsum("opix,oqjy->pqixjy", design, design, preferred_element_type=jnp.float32) * scale

time: 2140 us -> 2380 us (1.11)
  waiting for transfers between devices: 992 us -> 1460 us
  blocking collectives: 215 us -> 0 us
    all_gather x0 -> x1, waiting for transfers between devices: none -> 299 us  [on_device(): rhs = jnp.sum(lax.all_gather(rhs_local, ('gx', 'gy', 'gz')), 0)]
    psum x1 -> x0, blocking collectives: 215 us -> none  [on_device(): rhs = lax.psum(rhs_local, ('gx', 'gy', 'gz'))]
    all_gather x1, waiting for transfers between devices: 0.01 us -> 169 us  [on_device(): whole = lax.all_gather(across, 'gx', axis=0, tiled=True)]
  transfers between devices with their start and end apart: 36 -> 37, of which waited for: 35 -> 37; matrix products, arithmetic and copies ran while one was open for 0% -> 1% of each run, Pallas kernels for 0% -> 0%
where the time goes in v1:
time: 2380 us; the launch traced here: 2370 us
  waiting for transfers between devices  1460 us (61%)
  other arithmetic  542 us (23%)
  local copies, waits for them, and re-layouts  160 us (7%)
  matrix products  117 us (5%)
  starting transfers between devices  79.6 us (3%)
    all_gather x16, waiting for transfers between devices, picked(): lax.all_gather(x, axis)  366 us
    reduce_scatter x1, waiting for transfers between devices, on_device(): lax.psum_scatter(blockwise, ('gx', 'gy'), scatter_dimension=0, tiled=True)  312 us
    all_gather x1, waiting for transfers between devices, on_device(): rhs = jnp.sum(lax.all_gather(rhs_local, ('gx', 'gy', 'gz')), 0)  299 us
    all_to_all x16, waiting for transfers between devices, copy_for_each(): lax.all_to_all(jnp.broadcast_to(x[None], (size, *x.shape)), axis, 0, 0, t...  253 us
    another operation x48, other arithmetic, factor_step(): chol = jnp.linalg.cholesky(own_diag)  198 us
    another operation x3, other arithmetic, on_device(): jax.scipy.linalg.solve_triangular(lower, middle, lower=True, trans=1)  170 us
    all_gather x1, waiting for transfers between devices, on_device(): whole = lax.all_gather(across, 'gx', axis=0, tiled=True)  169 us
    another operation x32, other arithmetic, factor_step(): solved = jax.scipy.linalg.solve_triangular(chol, stacked, lower=True)  167 us
  transfers between devices with their start and end apart: 37, of which 37 were waited for; matrix products, arithmetic and copies ran while one was open for 1% of the time, Pallas kernels for 0%

profile of v1, /device:TPU:1, one launch (start us, length us, event | category | flops | bytes accessed | tf_op | source)
XLA Modules:
  0.0 2371.8 jit_solution(4316519583966928411)
XLA Ops:
  25.3 16.4 copy.39
  42.0 311.7 %reduce-scatter.2.cloned.1.call-done = f32[1,2,128,2,128]{4,2,3,1,0:T(8,128)} async-done(((f32[64,2,128,2,128]{4,2,3,1,0:T(8,128)}), f32[1,2,128,2,128]{4,2,3,1,0:T(8,128)}) %reduce-scatter.2.cloned.1.call-update) | async-done | bytes 262160 | tf_op jit(solution)/shard_map/reduce_scatter | solution.py:58
  353.8 35.4 %all-reduce.2.cloned.1.call-done = f32[2,128,2,128]{3,1,2,0:T(8,128)} async-done(((f32[2,128,2,128]{3,1,2,0:T(8,128)}), f32[2,128,2,128]{3,1,2,0:T(8,128)}) %all-reduce.2.cloned.1.call-update) | async-done | bytes 262160 | tf_op jit(solution)/shard_map/psum | solution.py:59
  389.2 1174.6 %while.20 = (s32[]{:T(128)}, f32[2,128,2,128]{3,1,2,0:T(8,128)}, f32[2,128,2,128]{3,1,0,2:T(8,128)S(1)}, s32[]{:T(128)}, s32[]{:T(128)}, /*index=5*/s32[]{:T(128...) while((s32[]{:T(128)}, f32[2,128,2,128]{3,1,2,0:T(8,128)}, ...), condition=%wide.region_5.6_spmd.clone, body=%wide.region_2.5_spmd.clone.sunk | while | flops 503890112 | bytes 12519428 | solution.py:104
  390.9 25.2 %all-gather.17.cloned.1.call-done = f32[16,128,1,128]{3,1,2,0:T(8,128)} async-done(((f32[2,128,1,128]{3,1,2,0:T(8,128)}), f32[16,128,1,128]{3,1,2,0:T(8,128)}) %all-gather.17.cloned.1.call-update) | async-done | bytes 1048592 | tf_op jit(solution)/shard_map/while/body/eval_jaxpr/all_gather | solution.py:11
  423.0 15.8 all-to-all-done
  466.6 22.6 all-gather.17.cloned.1.call-done
  539.8 22.6 all-gather.17.cloned.1.call-done
  612.9 22.6 all-gather.17.cloned.1.call-done
  642.5 15.8 all-to-all-done
  686.1 22.9 all-gather.17.cloned.1.call-done
  715.9 15.8 all-to-all-done
  759.6 22.9 all-gather.17.cloned.1.call-done
  833.0 22.9 all-gather.17.cloned.1.call-done
  906.5 22.6 all-gather.17.cloned.1.call-done
  979.7 22.9 all-gather.17.cloned.1.call-done
  1009.5 15.8 all-to-all-done
  1053.1 22.6 all-gather.17.cloned.1.call-done
  1082.6 15.8 all-to-all-done
  1126.3 22.9 all-gather.17.cloned.1.call-done
  1156.1 15.8 all-to-all-done
  1199.7 22.6 all-gather.17.cloned.1.call-done
  1272.9 22.6 all-gather.17.cloned.1.call-done
  1346.0 22.6 all-gather.17.cloned.1.call-done
  1419.2 22.6 all-gather.17.cloned.1.call-done
  1492.3 22.6 all-gather.17.cloned.1.call-done
  1569.4 20.6 all-gather.13.cloned.1.call-done
  1594.1 299.4 %all-gather.15.cloned.1.call-done = f32[2048,128]{1,0:T(8,128)} async-done(((f32[16,128]{1,0:T(8,128)}), f32[2048,128]{1,0:T(8,128)}) %all-gather.15.cloned.1.call-update) | async-done | bytes 1048592 | tf_op jit(solution)/shard_map/all_gather | solution.py:52
  1896.7 169.0 %all-gather.11.cloned.1.call-done = f32[8,2,128,8,2,128]{5,3,4,2,1,0:T(8,128)} async-done(((f32[1,2,128,8,2,128]{5,3,4,2,1,0:T(8,128)}), f32[8,2,128,8,2,128]{5,3,4,2,1,0:T(8,128)}) %all-gather.11.cloned.1.call-update) | async-done | bytes 16777232 | tf_op jit(solution)/shard_map/all_gather | solution.py:107
  2077.1 18.0 reshape.532
  2107.6 46.5 %while.19 = (s32[]{:T(128)}, f32[2048,2048]{1,0:T(8,128)}, s32[16,2]{0,1:T(2,128)S(1)}, f32[16,128,128]{2,1,0:T(8,128)S(1)}, s32[]{:T(128)}) while((s32[]{:T(128)}, f32[2048,2048]{1,0:T(8,128)}, s32[16,2]{0,1:T(2,128)S(1)}, f32[16,128,128]{2,1,0:T(8,128)S(1)}, s32[]{:T(128)}) %tuple.184), condition=%wide.while_cond, body=%wide.while_body.sunk | while | flops 2 | bytes 131181 | solution.py:110
  2154.1 157.2 %custom-call.28 = f32[16,128,128]{1,2,0:T(8,128)S(1)} custom-call(f32[16,128,128]{2,1,0:T(8,128)S(1)} %get-tuple-element.183), custom_call_target="InvertDiagBlocksLowerTriangular" | custom-call | tf_op jit(solution)/shard_map/jit(_solve_triangular)/triangular_solve | solution.py:110
  (576 shorter events, 866.5 us)
Async XLA Ops:
  7.2 346.6 %reduce-scatter.2.cloned.1.call-start = ((), (), s32[]{:S(2)}) async-start(), calls=%async_computation.2 | async-start | bytes 17039360 | tf_op jit(solution)/shard_map/reduce_scatter | solution.py:58
  41.8 347.4 %all-reduce.2.cloned.1.call-start = ((), (), s32[]{:S(2)}) async-start(), calls=%async_computation.3 | async-start | bytes 524288 | tf_op jit(solution)/shard_map/psum | solution.py:59
  389.2 26.9 %all-gather.17.cloned.1.call-start = ((), (), s32[]{:S(2)}) async-start(), calls=%async_computation.7 | async-start | bytes 1179648 | tf_op jit(solution)/shard_map/while/body/eval_jaxpr/all_gather | solution.py:11
  418.1 20.8 all-to-all-start
  465.0 24.3 %all-gather.17.cloned.1.call-start = ((), (), s32[]{:S(2)}) async-start(), calls=%async_computation.7 | async-start | bytes 1179648 | tf_op jit(solution)/shard_map/while/body/eval_jaxpr/all_gather | solution.py:11
  538.1 24.3 %all-gather.17.cloned.1.call-start = ((), (), s32[]{:S(2)}) async-start(), calls=%async_computation.7 | async-start | bytes 1179648 | tf_op jit(solution)/shard_map/while/body/eval_jaxpr/all_gather | solution.py:11
  611.3 24.3 %all-gather.17.cloned.1.call-start = ((), (), s32[]{:S(2)}) async-start(), calls=%async_computation.7 | async-start | bytes 1179648 | tf_op jit(solution)/shard_map/while/body/eval_jaxpr/all_gather | solution.py:11
  637.6 20.8 all-to-all-start
  684.4 24.6 %all-gather.17.cloned.1.call-start = ((), (), s32[]{:S(2)}) async-start(), calls=%async_computation.7 | async-start | bytes 1179648 | tf_op jit(solution)/shard_map/while/body/eval_jaxpr/all_gather | solution.py:11
  711.0 20.8 all-to-all-start
  757.9 24.6 %all-gather.17.cloned.1.call-start = ((), (), s32[]{:S(2)}) async-start(), calls=%async_computation.7 | async-start | bytes 1179648 | tf_op jit(solution)/shard_map/while/body/eval_jaxpr/all_gather | solution.py:11
  784.5 20.8 all-to-all-start
  831.4 24.6 %all-gather.17.cloned.1.call-start = ((), (), s32[]{:S(2)}) async-start(), calls=%async_computation.7 | async-start | bytes 1179648 | tf_op jit(solution)/shard_map/while/body/eval_jaxpr/all_gather | solution.py:11
  904.8 24.3 %all-gather.17.cloned.1.call-start = ((), (), s32[]{:S(2)}) async-start(), calls=%async_computation.7 | async-start | bytes 1179648 | tf_op jit(solution)/shard_map/while/body/eval_jaxpr/all_gather | solution.py:11
  978.0 24.6 %all-gather.17.cloned.1.call-start = ((), (), s32[]{:S(2)}) async-start(), calls=%async_computation.7 | async-start | bytes 1179648 | tf_op jit(solution)/shard_map/while/body/eval_jaxpr/all_gather | solution.py:11
  1004.6 20.8 all-to-all-start
  1051.4 24.3 %all-gather.17.cloned.1.call-start = ((), (), s32[]{:S(2)}) async-start(), calls=%async_computation.7 | async-start | bytes 1179648 | tf_op jit(solution)/shard_map/while/body/eval_jaxpr/all_gather | solution.py:11
  1077.7 20.8 all-to-all-start
  1124.6 24.6 %all-gather.17.cloned.1.call-start = ((), (), s32[]{:S(2)}) async-start(), calls=%async_computation.7 | async-start | bytes 1179648 | tf_op jit(solution)/shard_map/while/body/eval_jaxpr/all_gather | solution.py:11
  1151.2 20.8 all-to-all-start
  1198.1 24.3 %all-gather.17.cloned.1.call-start = ((), (), s32[]{:S(2)}) async-start(), calls=%async_computation.7 | async-start | bytes 1179648 | tf_op jit(solution)/shard_map/while/body/eval_jaxpr/all_gather | solution.py:11
  1224.3 20.8 all-to-all-start
  1271.2 24.3 %all-gather.17.cloned.1.call-start = ((), (), s32[]{:S(2)}) async-start(), calls=%async_computation.7 | async-start | bytes 1179648 | tf_op jit(solution)/shard_map/while/body/eval_jaxpr/all_gather | solution.py:11
  1297.5 20.8 all-to-all-start
  1344.4 24.3 %all-gather.17.cloned.1.call-start = ((), (), s32[]{:S(2)}) async-start(), calls=%async_computation.7 | async-start | bytes 1179648 | tf_op jit(solution)/shard_map/while/body/eval_jaxpr/all_gather | solution.py:11
  1370.6 20.8 all-to-all-start
  1417.5 24.3 %all-gather.17.cloned.1.call-start = ((), (), s32[]{:S(2)}) async-start(), calls=%async_computation.7 | async-start | bytes 1179648 | tf_op jit(solution)/shard_map/while/body/eval_jaxpr/all_gather | solution.py:11
  1490.7 24.3 %all-gather.17.cloned.1.call-start = ((), (), s32[]{:S(2)}) async-start(), calls=%async_computation.7 | async-start | bytes 1179648 | tf_op jit(solution)/shard_map/while/body/eval_jaxpr/all_gather | solution.py:11
  1517.0 20.8 all-to-all-start
  1563.8 26.1 %all-gather.13.cloned.1.call-start = ((), (), s32[]{:S(2)}) async-start(), calls=%async_computation.5 | async-start | bytes 2359296 | tf_op jit(solution)/shard_map/all_gather | solution.py:106
  1564.6 328.9 %all-gather.15.cloned.1.call-start = ((), (), s32[]{:S(2)}) async-start(), calls=%async_computation.6 | async-start | bytes 1056768 | tf_op jit(solution)/shard_map/all_gather | solution.py:52
  1569.1 496.6 %all-gather.11.cloned.1.call-start = ((), (), s32[]{:S(2)}) async-start(), calls=%async_computation.4 | async-start | bytes 18874368 | tf_op jit(solution)/shard_map/all_gather | solution.py:107
  (10 other events, 3634.5 us)
Sparse Core Ops, SparseCore 0:
  41.9 311.8 reduce-scatter.1
  356.2 32.9 all-reduce.1
  392.3 23.7 all-gather.16
  467.8 21.4 all-gather.16
  540.9 21.4 all-gather.16
  614.1 21.4 all-gather.16
  687.5 21.4 all-gather.16
  761.0 21.4 all-gather.16
  834.5 21.4 all-gather.16
  907.6 21.4 all-gather.16
  981.1 21.4 all-gather.16
  1054.2 21.4 all-gather.16
  1127.7 21.4 all-gather.16
  1200.8 21.4 all-gather.16
  1274.0 21.4 all-gather.16
  1347.2 21.4 all-gather.16
  1420.3 21.4 all-gather.16
  1493.5 21.4 all-gather.16
  1566.4 23.5 all-gather.12
  1592.0 301.4 all-gather.14
  1895.2 170.4 all-gather.10
